TPU v7x, 32 devices: a whole 2x2x4 slice. The times are simulated.
32 devices in a mesh: rows: 32 (over z, y, x, core).
Axes of the slice: x: 2, y: 2, z: 4, core: 2. Of those that a mesh axis runs over, the one named last changes fastest.
Arguments:
- left_factor: float32 [65536, 1024], P('rows'), may hold values from -6 to 6
- right_factor: float32 [65536, 1024], P('rows'), may hold values from -6 to 6
- tile_counts: int32 [32], P('rows'), may hold values from 1 to 4, as said below
- start_basis: float32 [1024, 256], replicated, may hold values from -6 to 6
Outputs:
- left_proj: float32 [65536, 256], P('rows')
- right_proj: float32 [65536, 256], P('rows')
Inputs may be any that keep to these rules, and one draw needn't show every extreme that they name: `tile_counts`: each device's live slots are its first ones; some device has 4 live slots and some device has 1.
All inputs are finite; a program needn't handle non-finite values.
Results may differ from a plain program's by a relative error of at most 0.0002.
Values sent between devices are 32-bit elements; how exact they have to be, the bound alone decides.
A program may use at most 128 MiB of HBM per device.

v0:
```python
import functools

import jax
import jax.numpy as jnp
from jax import lax
from jax.experimental import pallas as pl
from jax.experimental.pallas import tpu as pltpu
from jax.sharding import PartitionSpec as P

SLOTS = 4
POWER = 2
GROUP = 8
MESH = pl.DeviceIdType.MESH
NN = (((1,), (0,)), ((), ()))
NT = (((1,), (1,)), ((), ()))


def split(value):
    high = value.astype(jnp.bfloat16)
    return high, (value - high.astype(jnp.float32)).astype(jnp.bfloat16)


def dot_pairs(left, right, dims):
    one = lambda a, b: lax.dot_general(a, b, dims, preferred_element_type=jnp.float32)
    return one(left[0], right[0]) + (one(left[0], right[1]) + one(left[1], right[0]))


def full_dot(left, right, dims=NN):
    return lax.dot_general(
        left, right, dims, precision=lax.Precision.HIGHEST, preferred_element_type=jnp.float32
    )


def sum_kernel(chips, part, high, low, arrived, summed, gathered, total, d2d, rs, ag, fwd):
    me = lax.axis_index("rows")
    core = lax.rem(me, 2)
    chip = me // 2
    partner = me + 1 - 2 * core
    half = part.shape[0] // 2
    rows = half // chips

    def block(which, owner):
        return pl.ds(pl.multiple_of(which * half + owner * rows, GROUP), rows)

    def ahead(u):
        return lax.rem(chip + u, chips)

    def behind(u):
        return lax.rem(chip + chips - u, chips)

    def copy(src, dst, sems, u, device):
        return pltpu.make_async_remote_copy(
            src_ref=src,
            dst_ref=dst,
            send_sem=sems.at[0, u - 1],
            recv_sem=sems.at[1, u - 1],
            device_id=(device,),
            device_id_type=MESH,
        )

    def to_partner(u):
        return copy(part.at[block(1 - core, ahead(u))], arrived.at[u - 1], d2d, u, partner)

    def to_owner(u):
        return copy(summed.at[u - 1], gathered.at[u - 1], rs, u, 2 * ahead(u) + core)

    def to_peer(u):
        mine = block(core, chip)
        return copy(total.at[mine], total.at[mine], ag, u, 2 * ahead(u) + core)

    def from_peer(u):
        theirs = block(core, behind(u))
        return copy(total.at[theirs], total.at[theirs], ag, u, 2 * behind(u) + core)

    def pass_on(u):
        theirs = block(core, behind(u))
        return copy(total.at[theirs], total.at[theirs], fwd, u, partner)

    def from_partner(u):
        theirs = block(1 - core, behind(u))
        return copy(total.at[theirs], total.at[theirs], fwd, u, partner)

    def each(first, last, body):
        def step(u, carry):
            body(u)
            return carry

        lax.fori_loop(first, last, step, 0)

    def put(where):
        pair = split(total[where])
        high[where] = pair[0]
        low[where] = pair[1]

    barrier = pltpu.get_barrier_semaphore()
    pl.semaphore_signal(barrier, inc=1, device_id=(partner,), device_id_type=MESH)
    each(
        1,
        chips,
        lambda u: pl.semaphore_signal(
            barrier, inc=1, device_id=(2 * ahead(u) + core,), device_id_type=MESH
        ),
    )
    pl.semaphore_wait(barrier, chips)

    each(1, chips + 1, lambda u: to_partner(u).start())

    def reduce_pair(u):
        to_partner(u).wait_recv()
        summed[u - 1] = part[block(core, ahead(u))] + arrived[u - 1]
        to_owner(u).start()

    each(1, chips, reduce_pair)
    to_partner(chips).wait_recv()
    mine = block(core, chip)
    total[mine] = part[mine] + arrived[chips - 1]

    def accumulate(u):
        to_owner(u).wait_recv()
        total[mine] += gathered[u - 1]

    each(1, chips, accumulate)
    each(1, chips, lambda u: to_peer(u).start())
    pass_on(chips).start()
    put(mine)

    def relay(u):
        from_peer(u).wait_recv()
        pass_on(u).start()
        put(block(core, behind(u)))

    each(1, chips, relay)
    from_partner(chips).wait_recv()
    put(block(1 - core, chip))

    def take(u):
        from_partner(u).wait_recv()
        put(block(1 - core, behind(u)))

    each(1, chips, take)
    each(1, chips + 1, lambda u: to_partner(u).wait_send())
    each(1, chips, lambda u: to_owner(u).wait_send())
    each(1, chips, lambda u: to_peer(u).wait_send())
    each(1, chips + 1, lambda u: pass_on(u).wait_send())


def sum_over_devices(part, devices):
    chips = devices // 2
    size, width = part.shape
    rows = size // devices
    block = pltpu.VMEM((chips, rows, width), jnp.float32)
    vmem = pl.BlockSpec(memory_space=pltpu.VMEM)
    sems = pltpu.SemaphoreType.DMA((2, chips))
    return pl.pallas_call(
        functools.partial(sum_kernel, chips),
        out_shape=[jax.ShapeDtypeStruct(part.shape, jnp.bfloat16)] * 2,
        in_specs=[vmem],
        out_specs=[vmem, vmem],
        scratch_shapes=[block, block, block, pltpu.VMEM(part.shape, jnp.float32), sems, sems, sems, sems],
        compiler_params=pltpu.CompilerParams(
            collective_id=0, has_side_effects=True, vmem_limit_bytes=40 * 2**20
        ),
        name="sum_over_devices",
    )(part)


def inverse_factor(matrix):
    size = matrix.shape[0]
    groups = size // GROUP
    shape = (GROUP, size)
    row_ids = lax.broadcasted_iota(jnp.int32, shape, 0)
    lane_ids = lax.broadcasted_iota(jnp.int32, shape, 1)
    wide = lambda v: jnp.broadcast_to(v, shape)
    left = [matrix[GROUP * g : GROUP * (g + 1), :] for g in range(groups)]
    right = [jnp.where(lane_ids == row_ids + GROUP * g, 1.0, 0.0) for g in range(groups)]
    for g in range(groups):
        panel, beside = left[g], right[g]
        entry, factor, inverse, scale = {}, {}, {}, {}
        for j in range(GROUP):
            column = wide(panel[:, GROUP * g + j : GROUP * g + j + 1])
            for i in range(j, GROUP):
                entry[i, j] = wide(column[i : i + 1, :])
        for j in range(GROUP):
            scale[j] = lax.rsqrt(entry[j, j])
            for i in range(j + 1, GROUP):
                factor[i, j] = entry[i, j] * scale[j]
            for l in range(j + 1, GROUP):
                for i in range(l, GROUP):
                    entry[i, l] = entry[i, l] - factor[i, j] * factor[l, j]
        for j in range(GROUP):
            inverse[j, j] = scale[j]
            for i in range(j + 1, GROUP):
                acc = factor[i, j] * inverse[j, j]
                for l in range(j + 1, i):
                    acc = acc + factor[i, l] * inverse[l, j]
                inverse[i, j] = -acc * scale[i]
        new_panel, new_beside = jnp.zeros(shape, jnp.float32), jnp.zeros(shape, jnp.float32)
        for j in range(GROUP):
            column = jnp.zeros(shape, jnp.float32)
            for i in range(j, GROUP):
                column = jnp.where(row_ids == i, inverse[i, j], column)
            new_panel = new_panel + column * wide(panel[j : j + 1, :])
            new_beside = new_beside + column * wide(beside[j : j + 1, :])
        right[g] = new_beside
        if g + 1 < groups:
            turned = new_panel.T
            rows_of = [wide(new_panel[j : j + 1, :]) for j in range(GROUP)]
            beside_of = [wide(new_beside[j : j + 1, :]) for j in range(GROUP)]
            for r in range(g + 1, groups):
                tile = turned[GROUP * r : GROUP * (r + 1), :]
                for j in range(GROUP):
                    weight = wide(tile[:, j : j + 1])
                    left[r] = left[r] - weight * rows_of[j]
                    right[r] = right[r] - weight * beside_of[j]
    return jnp.concatenate(right, axis=0)


def chain_kernel(start, high, low, left_map, right_map, basis, image, square, inverse):
    rank = start.shape[0]
    cut = rank // 2
    basis[...] = start[...]
    inverse[...] = jnp.zeros_like(inverse)

    def turn(iteration, carry):
        gram = (high[...], low[...])
        image[...] = dot_pairs(split(basis[...]), gram, NT)

        @pl.when(iteration < POWER)
        def _():
            image[...] = dot_pairs(split(image[...]), (high[...], low[...]), NN)

        pair = split(image[...])
        square[...] = dot_pairs(pair, pair, NT)
        first = inverse_factor(square[:cut, :cut])
        across = full_dot(first, square[:cut, cut:])
        across_t = across.T
        second = inverse_factor(square[cut:, cut:] - full_dot(across_t, across))
        inverse[:cut, :cut] = first
        inverse[cut:, cut:] = second
        inverse[cut:, :cut] = -full_dot(second, full_dot(across_t, first))
        solved = split(inverse[...])

        @pl.when(iteration == POWER)
        def _():
            shape = square.shape
            diagonal = lax.broadcasted_iota(jnp.int32, shape, 0) == lax.broadcasted_iota(jnp.int32, shape, 1)
            trace = jnp.sum(jnp.where(diagonal, square[...], 0.0), keepdims=True)
            scaling = jnp.sqrt(trace / rank)
            right_map[...] = dot_pairs(solved, split(basis[...]), NN) * scaling
            left_map[...] = dot_pairs(solved, pair, NN)

        @pl.when(iteration < POWER)
        def _():
            basis[...] = dot_pairs(solved, pair, NN)

        return carry

    lax.fori_loop(0, POWER + 1, turn, 0)


def maps_of(start_rows, high, low):
    rank, states = start_rows.shape
    vmem = pl.BlockSpec(memory_space=pltpu.VMEM)
    small = pltpu.VMEM((rank, rank), jnp.float32)
    wide = pltpu.VMEM((rank, states), jnp.float32)
    return pl.pallas_call(
        chain_kernel,
        out_shape=[jax.ShapeDtypeStruct((rank, states), jnp.float32)] * 2,
        in_specs=[vmem] * 3,
        out_specs=[vmem] * 2,
        scratch_shapes=[wide, wide, small, small],
        compiler_params=pltpu.CompilerParams(vmem_limit_bytes=40 * 2**20),
        name="maps_of",
    )(start_rows, high, low)


def project(factor_rows, mapping, row_mask):
    rows = lax.dot_general(
        factor_rows, mapping, NT, precision=lax.Precision.HIGH, preferred_element_type=jnp.float32
    )
    return rows * row_mask


def local(devices, left_factor, right_factor, tile_counts, start_basis):
    tile_rows = left_factor.shape[0] // SLOTS
    live_count = tile_counts[0]
    slot_ids = lax.broadcasted_iota(jnp.int32, (SLOTS, 1, 1), 0)
    live_slots = (slot_ids < live_count).astype(jnp.float32)
    row_mask = jnp.broadcast_to(live_slots, (SLOTS, tile_rows, 1)).reshape(-1, 1)
    part = lax.dot_general(
        left_factor,
        right_factor * row_mask,
        (((0,), (0,)), ((), ())),
        precision=lax.Precision.HIGH,
        preferred_element_type=jnp.float32,
    )
    high, low = sum_over_devices(part, devices)
    left_map, right_map = maps_of(start_basis.T, high, low)
    return project(left_factor, left_map, row_mask), project(right_factor, right_map, row_mask)


def solution(mesh):
    return jax.shard_map(
        functools.partial(local, mesh.shape["rows"]),
        mesh=mesh,
        in_specs=(P("rows", None), P("rows", None), P("rows"), P()),
        out_specs=(P("rows", None), P("rows", None)),
        check_vma=False,
    )
```

profile of v0, /device:TPU:31, one launch (start us, length us, event | category | flops | bytes accessed | tf_op | source)
XLA Modules:
  0.0 209.4 jit_solution(1103586273838864151)
XLA Ops:
  1.3 0.1 broadcast_bitcast_fusion
  1.4 18.6 %fusion.5.part = f32[1024,1024]{1,0:T(8,128)S(1)} fusion(f32[2048,1024]{1,0:T(8,128)} %param.4, f32[2048,1024]{1,0:T(8,128)} %param.5, f32[2048]{0:T(1024)S(1)} %bitcast.18), kind=kOutput, calls=%fused_computation.7 | convolution fusion | flops 12886999040 | bytes 20979712 | tf_op jit(solution)/shard_map/dot_general | solution.py:290
  19.9 115.1 %sum_over_devices.1 = (bf16[1024,1024]{1,0:T(8,128)(2,1)S(1)}, bf16[1024,1024]{1,0:T(8,128)(2,1)S(1)}) custom-call(f32[1024,1024]{1,0:T(8,128)S(1)} %fusion.5.part), custom_call_target="tpu_custom_call" | custom-call | tf_op jit(solution)/shard_map/sum_over_devices/pallas_call | solution.py:154
  135.0 0.0 copy-start
  135.0 1.3 copy-done
  136.3 1.6 copy.6
  137.9 0.0 copy-start.1
  137.9 1.6 copy-done.1
  139.5 53.2 %maps_of.1 = (f32[256,1024]{1,0:T(8,128)S(1)}, f32[256,1024]{1,0:T(8,128)S(1)}) custom-call(f32[256,1024]{1,0:T(8,128)S(1)} %bitcast.17, bf16[1024,1024]{1,0:T(8,128)(2,1)S(1)} %get-tuple-element.6.high, bf16[1024,1024]{1,0:T(8,128)(2,1)S(1)} %copy-done.1), custom_call_target="tpu_custom_call" | custom-call | tf_op jit(solution)/shard_map/maps_of/pallas_call | solution.py:266
  192.6 0.0 copy-start.2
  192.6 1.0 copy-done.2
  193.6 0.0 copy-start.3
  193.6 6.1 %fusion.3 = f32[2048,256]{0,1:T(8,128)S(1)} fusion(f32[256,1024]{1,0:T(8,128)S(1)} %get-tuple-element.9, f32[2048,1024]{1,0:T(8,128)} %param.5, f32[2048]{0:T(1024)S(1)} %bitcast.19), kind=kOutput, calls=%fused_computation.4 | convolution fusion | flops 3221749760 | bytes 11542528 | tf_op jit(solution)/shard_map/dot_general | solution.py:278
  199.8 1.8 copy.9
  201.6 0.0 copy-done.3
  201.6 6.0 %fusion.4 = f32[2048,256]{0,1:T(8,128)S(1)} fusion(f32[256,1024]{1,0:T(8,128)S(1)} %copy-done.3, f32[2048,1024]{1,0:T(8,128)} %param.4, f32[2048]{0:T(1024)S(1)} %bitcast.20), kind=kOutput, calls=%fused_computation.6 | convolution fusion | flops 3221749760 | bytes 11542528 | tf_op jit(solution)/shard_map/dot_general | solution.py:278
  207.6 1.8 copy.8
  (2 shorter events, 0.0 us)
Async XLA Ops:
  135.0 1.3 copy-start
  137.9 1.6 copy-start.1
  192.6 1.0 copy-start.2
  193.6 8.0 %copy-start.3 = (f32[256,1024]{1,0:T(8,128)S(1)}, f32[256,1024]{1,0:T(8,128)}, u32[]{:S(2)}) copy-start(f32[256,1024]{1,0:T(8,128)} %copy-done.2) | copy-start | bytes 3145732
where the time goes:
time: 210 us; the launch traced here: 209 us
  Pallas kernels  168 us (80%)
  matrix products  30.7 us (15%)
  local copies, waits for them, and re-layouts  9.13 us (4%)
    pallas_call x1, Pallas kernels, sum_over_devices(): pl.pallas_call(functools.partial(sum_kernel, chips), out_shape=[jax.Shape...  115 us
    pallas_call x1, Pallas kernels, maps_of(): pl.pallas_call(chain_kernel, out_shape=[jax.ShapeDtypeStruct((rank, state...  53.2 us
    dot_general x1, matrix products, local(): lax.dot_general(left_factor, right_factor * row_mask, (((0,), (0,)), ((),...  18.6 us
    dot_general x2, matrix products, project(): lax.dot_general(factor_rows, mapping, NT, precision=lax.Precision.HIGH, p...  12.2 us
    unnamed x13, local copies, waits for them, and re-layouts  9.13 us

commit v1 on v0

--- a/solution.py
+++ b/solution.py
@@ -10,6 +10,7 @@
 SLOTS = 4
 POWER = 2
 GROUP = 8
+LANES = 128
 MESH = pl.DeviceIdType.MESH
 NN = (((1,), (0,)), ((), ()))
 NT = (((1,), (1,)), ((), ()))
@@ -31,135 +32,234 @@
     )
 
 
-def sum_kernel(chips, part, high, low, arrived, summed, gathered, total, d2d, rs, ag, fwd):
+def grid_of(chips):
+    bits = chips.bit_length() - 1
+    inner = bits // 3
+    middle = (bits - inner) // 2
+    sizes = (2**inner, 2**middle, chips // 2 ** (inner + middle))
+    return sizes
+
+
+class Route:
+    def __init__(self, chip, core, axes, half, flip):
+        self.half = half
+        self.sizes = [s for s, _ in axes]
+        self.strides = [d for _, d in axes]
+        self.digits = [lax.rem(chip // d, s) for s, d in axes]
+        self.rows = [half]
+        self.first = [0]
+        for s, a in zip(self.sizes, self.digits):
+            self.rows.append(self.rows[-1] // s)
+            self.first.append(self.first[-1] + a * self.rows[-1])
+
+def sum_kernel(chips, lags, part, high, low, *scratch):
+    arrived, acc, total = scratch[:3]
+    p_in, q_in = scratch[3:6], scratch[6:9]
+    d2d, fwd = scratch[9:11]
+    rs, ag = scratch[11:14], scratch[14:17]
+    qrs, qag = scratch[17:20], scratch[20:23]
     me = lax.axis_index("rows")
     core = lax.rem(me, 2)
     chip = me // 2
     partner = me + 1 - 2 * core
     half = part.shape[0] // 2
-    rows = half // chips
-
-    def block(which, owner):
-        return pl.ds(pl.multiple_of(which * half + owner * rows, GROUP), rows)
-
-    def ahead(u):
-        return lax.rem(chip + u, chips)
-
-    def behind(u):
-        return lax.rem(chip + chips - u, chips)
-
-    def copy(src, dst, sems, u, device):
-        return pltpu.make_async_remote_copy(
-            src_ref=src,
-            dst_ref=dst,
-            send_sem=sems.at[0, u - 1],
-            recv_sem=sems.at[1, u - 1],
-            device_id=(device,),
-            device_id_type=MESH,
-        )
-
-    def to_partner(u):
-        return copy(part.at[block(1 - core, ahead(u))], arrived.at[u - 1], d2d, u, partner)
-
-    def to_owner(u):
-        return copy(summed.at[u - 1], gathered.at[u - 1], rs, u, 2 * ahead(u) + core)
-
-    def to_peer(u):
-        mine = block(core, chip)
-        return copy(total.at[mine], total.at[mine], ag, u, 2 * ahead(u) + core)
-
-    def from_peer(u):
-        theirs = block(core, behind(u))
-        return copy(total.at[theirs], total.at[theirs], ag, u, 2 * behind(u) + core)
-
-    def pass_on(u):
-        theirs = block(core, behind(u))
-        return copy(total.at[theirs], total.at[theirs], fwd, u, partner)
-
-    def from_partner(u):
-        theirs = block(1 - core, behind(u))
-        return copy(total.at[theirs], total.at[theirs], fwd, u, partner)
-
-    def each(first, last, body):
+    chunks = part.shape[1] // LANES
+    kx, ky, kz = grid_of(chips)
+    flat = kx == ky
+    def pick(c, a, b):
+        return a + c * (b - a) if flat else a
+    def axes(c, z_first):
+        plane = [(kx, pick(c, 1, kx)), (ky, pick(c, kx, 1))]
+        line = (kz, kx * ky)
+        return [line] + plane if z_first else plane + [line]
+    mine = {z: Route(chip, core, axes(core, z), half, 0) for z in (False, True)}
+    theirs = {z: Route(chip, core, axes(1 - core, z), half, 0) for z in (False, True)}
+
+    def lanes(c):
+        return pl.ds(c * LANES if isinstance(c, int) else pl.multiple_of(c * LANES, LANES), LANES)
+    def rows(start, count, base=0):
+        return pl.ds(pl.multiple_of(base + start, GROUP), count)
+    def copy(src, dst, send, recv, device):
+        return pltpu.make_async_remote_copy(src_ref=src, dst_ref=dst, send_sem=send, recv_sem=recv, device_id=(device,), device_id_type=MESH)
+
+    last = chunks - 1
+    my_base, its_base = core * half, (1 - core) * half
+
+    def to_partner(c):
+        return copy(part.at[rows(0, half, its_base), lanes(c)], arrived.at[c], d2d.at[0, c], d2d.at[1, c], partner)
+
+    def peer(r, p, step):
+        digit = lax.rem(r.digits[p] + step + r.sizes[p], r.sizes[p])
+        return digit, 2 * (chip + (digit - r.digits[p]) * r.strides[p]) + core
+
+    def rs_copy(z, p, c, u):
+        r = mine[z]
+        digit, device = peer(r, p, u)
+        n = r.rows[p + 1]
+        sems = (qrs if z else rs)[p]
+        box = (q_in if z else p_in)[p]
+        slot = 0 if z else c
+        return copy(acc.at[c, rows(r.first[p] + digit * n, n)], box.at[slot, u - 1], sems.at[0, slot, u - 1], sems.at[1, slot, u - 1], device)
+
+    def ag_copy(z, p, c, u, outgoing):
+        r = mine[z]
+        n = r.rows[p + 1]
+        digit, device = peer(r, p, u if outgoing else -u)
+        where = rows(r.first[p + 1] if outgoing else r.first[p] + digit * n, n, my_base)
+        sems = (qag if z else ag)[p]
+        slot = 0 if z else c
+        return copy(total.at[c, where], total.at[c, where], sems.at[0, slot, u - 1], sems.at[1, slot, u - 1], device)
+
+    def pieces(r, base):
+        out = [rows(r.first[2], r.rows[2], base)]
+        for p in (1, 0):
+            for u in range(1, r.sizes[p]):
+                digit = lax.rem(r.digits[p] - u + r.sizes[p], r.sizes[p])
+                out.append(rows(r.first[p] + digit * r.rows[p + 1], r.rows[p + 1], base))
+        return out
+
+    def pass_on(z, c, i, outgoing):
+        where = pieces(mine[z] if outgoing else theirs[z], my_base if outgoing else its_base)[i]
+        return copy(total.at[c, where], total.at[c, where], fwd.at[0, c, i], fwd.at[1, c, i], partner)
+
+    def put(c, where):
+        pair = split(total[c, where, :])
+        high[where, lanes(c)] = pair[0]
+        low[where, lanes(c)] = pair[1]
+
+    def rs_start(z, p, c):
+        for u in range(1, mine[z].sizes[p]):
+            rs_copy(z, p, c, u).start()
+
+    def rs_finish(z, p, c):
+        r = mine[z]
+        for u in range(1, r.sizes[p]):
+            rs_copy(z, p, c, u).wait_recv()
+        where = rows(r.first[p + 1], r.rows[p + 1])
+        box = (q_in if z else p_in)[p]
+        slot = 0 if z else c
+        value = acc[c, where, :]
+        for u in range(1, r.sizes[p]):
+            value += box[slot, u - 1]
+        if p == 2:
+            total[c, rows(r.first[3], r.rows[3], my_base), :] = value
+        else:
+            acc[c, where, :] = value
+
+    def ag_start(z, p, c):
+        for u in range(1, mine[z].sizes[p]):
+            ag_copy(z, p, c, u, True).start()
+
+    def ag_finish(z, p, c):
+        for u in range(1, mine[z].sizes[p]):
+            ag_copy(z, p, c, u, False).wait_recv()
+
+    def event(kind, z, c):
+        if kind == "D":
+            to_partner(c).wait_recv()
+            acc[c] = part[rows(0, half, my_base), lanes(c)] + arrived[c]
+            rs_start(z, 0, c)
+        elif kind in ("F1", "F2"):
+            p = int(kind[1]) - 1
+            rs_finish(z, p, c)
+            rs_start(z, p + 1, c)
+        elif kind == "F3":
+            rs_finish(z, 2, c)
+            ag_start(z, 2, c)
+        elif kind == "A3":
+            ag_finish(z, 2, c)
+            ag_start(z, 1, c)
+            pass_on(z, c, 0, True).start()
+            put(c, pieces(mine[z], my_base)[0])
+        elif kind == "A2":
+            ag_finish(z, 1, c)
+            ag_start(z, 0, c)
+            for u in range(1, mine[z].sizes[1]):
+                pass_on(z, c, u, True).start()
+                put(c, pieces(mine[z], my_base)[u])
+        elif kind == "A1":
+            ag_finish(z, 0, c)
+            for u in range(1, mine[z].sizes[0]):
+                i = u + mine[z].sizes[1] - 1
+                pass_on(z, c, i, True).start()
+                put(c, pieces(mine[z], my_base)[i])
+        else:
+            for i, where in enumerate(pieces(theirs[z], its_base)):
+                pass_on(z, c, i, False).wait_recv()
+                put(c, where)
+
+    def each(first, end, body):
         def step(u, carry):
             body(u)
             return carry
-
-        lax.fori_loop(first, last, step, 0)
-
-    def put(where):
-        pair = split(total[where])
-        high[where] = pair[0]
-        low[where] = pair[1]
+        lax.fori_loop(first, end, step, 0)
 
     barrier = pltpu.get_barrier_semaphore()
+    devices = {}
     pl.semaphore_signal(barrier, inc=1, device_id=(partner,), device_id_type=MESH)
-    each(
-        1,
-        chips,
-        lambda u: pl.semaphore_signal(
-            barrier, inc=1, device_id=(2 * ahead(u) + core,), device_id_type=MESH
-        ),
-    )
-    pl.semaphore_wait(barrier, chips)
-
-    each(1, chips + 1, lambda u: to_partner(u).start())
-
-    def reduce_pair(u):
-        to_partner(u).wait_recv()
-        summed[u - 1] = part[block(core, ahead(u))] + arrived[u - 1]
-        to_owner(u).start()
-
-    each(1, chips, reduce_pair)
-    to_partner(chips).wait_recv()
-    mine = block(core, chip)
-    total[mine] = part[mine] + arrived[chips - 1]
-
-    def accumulate(u):
-        to_owner(u).wait_recv()
-        total[mine] += gathered[u - 1]
-
-    each(1, chips, accumulate)
-    each(1, chips, lambda u: to_peer(u).start())
-    pass_on(chips).start()
-    put(mine)
-
-    def relay(u):
-        from_peer(u).wait_recv()
-        pass_on(u).start()
-        put(block(core, behind(u)))
-
-    each(1, chips, relay)
-    from_partner(chips).wait_recv()
-    put(block(1 - core, chip))
-
-    def take(u):
-        from_partner(u).wait_recv()
-        put(block(1 - core, behind(u)))
-
-    each(1, chips, take)
-    each(1, chips + 1, lambda u: to_partner(u).wait_send())
-    each(1, chips, lambda u: to_owner(u).wait_send())
-    each(1, chips, lambda u: to_peer(u).wait_send())
-    each(1, chips + 1, lambda u: pass_on(u).wait_send())
-
-
-def sum_over_devices(part, devices):
+    count = 1
+    for p in range(3):
+        for u in range(1, mine[False].sizes[p]):
+            pl.semaphore_signal(barrier, inc=1, device_id=(peer(mine[False], p, u)[1],), device_id_type=MESH)
+            count += 1
+    pl.semaphore_wait(barrier, count)
+
+    to_partner(last).start()
+    each(0, last, lambda c: to_partner(c).start())
+    event("D", True, last)
+    each(0, last, lambda c: event("D", False, c))
+
+    q_lags = lags["Q"]
+    end = 1 + max(last - 1 + max(v for k, v in lags.items() if k != "Q"), max(q_lags.values()))
+    def step(t):
+        for kind in ("F1", "F2", "F3", "A3", "A2", "A1", "W"):
+            c = t - lags[kind]
+            pl.when((c >= 0) & (c < last))(functools.partial(event, kind, False, c))
+            pl.when(t == q_lags[kind])(functools.partial(event, kind, True, last))
+    each(0, end, step)
+
+    def drain(z, c):
+        to_partner(c).wait_send()
+        for p in range(3):
+            for u in range(1, mine[z].sizes[p]):
+                rs_copy(z, p, c, u).wait_send()
+                ag_copy(z, p, c, u, True).wait_send()
+        for i in range(len(pieces(mine[z], my_base))):
+            pass_on(z, c, i, True).wait_send()
+    each(0, last, lambda c: drain(False, c))
+    drain(True, last)
+
+LAGS = dict(F1=0, F2=1, F3=3, A3=5, A2=7, A1=9, W=10, Q=dict(F1=3, F2=4, F3=5, A3=7, A2=8, A1=12, W=13))
+
+def sum_over_devices(part, devices, lags=LAGS):
     chips = devices // 2
     size, width = part.shape
-    rows = size // devices
-    block = pltpu.VMEM((chips, rows, width), jnp.float32)
+    half = size // 2
+    chunks = width // LANES
+    kx, ky, kz = grid_of(chips)
     vmem = pl.BlockSpec(memory_space=pltpu.VMEM)
-    sems = pltpu.SemaphoreType.DMA((2, chips))
+    dma = pltpu.SemaphoreType.DMA
+    def boxes(order, slots):
+        left, out = half, []
+        for k in order:
+            left //= k
+            out.append(pltpu.VMEM((slots, k - 1, left, LANES), jnp.float32))
+        return out
+    def sems(order, slots):
+        return [dma((2, slots, k - 1)) for k in order]
+    p_order, q_order = (kx, ky, kz), (kz, kx, ky)
+    scratch = [pltpu.VMEM((chunks, half, LANES), jnp.float32)] * 2 + [pltpu.VMEM((chunks, size, LANES), jnp.float32)]
+    scratch += boxes(p_order, chunks - 1) + boxes(q_order, 1)
+    fw = max(kx + ky - 1, kz + kx - 1)
+    scratch += [dma((2, chunks)), dma((2, chunks, fw))]
+    scratch += sems(p_order, chunks - 1) * 2 + sems(q_order, 1) * 2
     return pl.pallas_call(
-        functools.partial(sum_kernel, chips),
+        functools.partial(sum_kernel, chips, lags),
         out_shape=[jax.ShapeDtypeStruct(part.shape, jnp.bfloat16)] * 2,
         in_specs=[vmem],
         out_specs=[vmem, vmem],
-        scratch_shapes=[block, block, block, pltpu.VMEM(part.shape, jnp.float32), sems, sems, sems, sems],
-        compiler_params=pltpu.CompilerParams(
-            collective_id=0, has_side_effects=True, vmem_limit_bytes=40 * 2**20
-        ),
+        scratch_shapes=scratch,
+        compiler_params=pltpu.CompilerParams(collective_id=0, has_side_effects=True, vmem_limit_bytes=48 * 2**20),
         name="sum_over_devices",
     )(part)
 

time: 210 us -> 152 us (0.72)
  the two profiles are of different devices: /device:TPU:31 before, /device:TPU:1 now
where the time goes in v1:
time: 152 us
  Pallas kernels  109 us (72%)
  matrix products  32.4 us (21%)
  local copies, waits for them, and re-layouts  9.13 us (6%)
    pallas_call x1, Pallas kernels, sum_over_devices(): pl.pallas_call(functools.partial(sum_kernel, chips, lags), out_shape=[jax...  56.1 us
    pallas_call x1, Pallas kernels, maps_of(): pl.pallas_call(chain_kernel, out_shape=[jax.ShapeDtypeStruct((rank, state...  53.1 us
    dot_general x1, matrix products, local(): lax.dot_general(left_factor, right_factor * row_mask, (((0,), (0,)), ((),...  20.2 us
    dot_general x2, matrix products, project(): lax.dot_general(factor_rows, mapping, NT, precision=lax.Precision.HIGH, p...  12.2 us
    unnamed x13, local copies, waits for them, and re-layouts  9.13 us

profile of v1, /device:TPU:1, one launch (start us, length us, event | category | flops | bytes accessed | tf_op | source)
XLA Modules:
  0.0 152.1 jit_solution(4018096219711707332)
XLA Ops:
  1.3 0.1 broadcast_bitcast_fusion
  1.4 20.2 %fusion.5.part = f32[1024,1024]{1,0:T(8,128)} fusion(f32[2048,1024]{1,0:T(8,128)} %param.4, f32[2048,1024]{1,0:T(8,128)} %param.5, f32[2048]{0:T(1024)S(1)} %bitcast.18), kind=kOutput, calls=%fused_computation.7 | convolution fusion | flops 12886999040 | bytes 20979712 | tf_op jit(solution)/shard_map/dot_general | solution.py:390
  21.6 56.1 %sum_over_devices.1 = (bf16[1024,1024]{1,0:T(8,128)(2,1)S(1)}, bf16[1024,1024]{1,0:T(8,128)(2,1)S(1)}) custom-call(f32[1024,1024]{1,0:T(8,128)} %fusion.5.part), custom_call_target="tpu_custom_call" | custom-call | tf_op jit(solution)/shard_map/sum_over_devices/pallas_call | solution.py:256
  77.7 0.0 copy-start
  77.7 1.3 copy-done
  79.0 1.6 %copy.6 = f32[1024,256]{0,1:T(8,128)S(1)} copy(f32[1024,256]{1,0:T(8,128)} %param.7) | data formatting | bytes 2097152 | tf_op args[3]
  80.6 0.0 copy-start.1
  80.6 1.6 %copy-done.1 = bf16[1024,1024]{1,0:T(8,128)(2,1)S(1)} copy-done((bf16[1024,1024]{1,0:T(8,128)(2,1)S(1)}, bf16[1024,1024]{1,0:T(8,128)(2,1)}, u32[]{:S(2)}) %copy-start.1) | copy-done | bytes 2097176
  82.2 53.1 %maps_of.1 = (f32[256,1024]{1,0:T(8,128)S(1)}, f32[256,1024]{1,0:T(8,128)S(1)}) custom-call(f32[256,1024]{1,0:T(8,128)S(1)} %bitcast.17, bf16[1024,1024]{1,0:T(8,128)(2,1)S(1)} %get-tuple-element.6.high, bf16[1024,1024]{1,0:T(8,128)(2,1)S(1)} %copy-done.1), custom_call_target="tpu_custom_call" | custom-call | tf_op jit(solution)/shard_map/maps_of/pallas_call | solution.py:366
  135.3 0.0 copy-start.2
  135.4 1.0 copy-done.2
  136.3 0.0 copy-start.3
  136.3 6.1 %fusion.3 = f32[2048,256]{0,1:T(8,128)S(1)} fusion(f32[256,1024]{1,0:T(8,128)S(1)} %get-tuple-element.9, f32[2048,1024]{1,0:T(8,128)} %param.5, f32[2048]{0:T(1024)S(1)} %bitcast.19), kind=kOutput, calls=%fused_computation.4 | convolution fusion | flops 3221749760 | bytes 11542528 | tf_op jit(solution)/shard_map/dot_general | solution.py:378
  142.5 1.8 %copy.9 = f32[2048,256]{1,0:T(8,128)} copy(f32[2048,256]{0,1:T(8,128)S(1)} %fusion.3) | data formatting | bytes 4194304
  144.3 0.0 copy-done.3
  144.3 6.0 %fusion.4 = f32[2048,256]{0,1:T(8,128)S(1)} fusion(f32[256,1024]{1,0:T(8,128)S(1)} %copy-done.3, f32[2048,1024]{1,0:T(8,128)} %param.4, f32[2048]{0:T(1024)S(1)} %bitcast.20), kind=kOutput, calls=%fused_computation.6 | convolution fusion | flops 3221749760 | bytes 11542528 | tf_op jit(solution)/shard_map/dot_general | solution.py:378
  150.3 1.8 %copy.8 = f32[2048,256]{1,0:T(8,128)} copy(f32[2048,256]{0,1:T(8,128)S(1)} %fusion.4) | data formatting | bytes 4194304
  (2 shorter events, 0.0 us)
Async XLA Ops:
  77.7 1.3 copy-start
  80.6 1.6 %copy-start.1 = (bf16[1024,1024]{1,0:T(8,128)(2,1)S(1)}, bf16[1024,1024]{1,0:T(8,128)(2,1)}, u32[]{:S(2)}) copy-start(bf16[1024,1024]{1,0:T(8,128)(2,1)} %copy-done) | copy-start | bytes 6291460
  135.3 1.0 copy-start.2
  136.3 8.0 %copy-start.3 = (f32[256,1024]{1,0:T(8,128)S(1)}, f32[256,1024]{1,0:T(8,128)}, u32[]{:S(2)}) copy-start(f32[256,1024]{1,0:T(8,128)} %copy-done.2) | copy-start | bytes 3145732

commit v2 on v1

v2 whole, which is shorter than its diff:
```python
import functools

import jax
import jax.numpy as jnp
from jax import lax
from jax.experimental import pallas as pl
from jax.experimental.pallas import tpu as pltpu
from jax.sharding import PartitionSpec as P

SLOTS = 4
POWER = 2
GROUP = 8
LANES = 128
PANEL = 256
MESH = pl.DeviceIdType.MESH
NN = (((1,), (0,)), ((), ()))
NT = (((1,), (1,)), ((), ()))


def split(value):
    high = value.astype(jnp.bfloat16)
    return high, (value - high.astype(jnp.float32)).astype(jnp.bfloat16)


def dot_pairs(left, right, dims):
    one = lambda a, b: lax.dot_general(a, b, dims, preferred_element_type=jnp.float32)
    return one(left[0], right[0]) + (one(left[0], right[1]) + one(left[1], right[0]))


def full_dot(left, right, dims=NN):
    return lax.dot_general(
        left, right, dims, precision=lax.Precision.HIGHEST, preferred_element_type=jnp.float32
    )


def grid_of(chips):
    bits = chips.bit_length() - 1
    inner = bits // 3
    middle = (bits - inner) // 2
    sizes = (2**inner, 2**middle, chips // 2 ** (inner + middle))
    return sizes


class Route:
    def __init__(self, chip, core, axes, half, flip):
        self.half = half
        self.sizes = [s for s, _ in axes]
        self.strides = [d for _, d in axes]
        self.digits = [lax.rem(chip // d, s) for s, d in axes]
        self.rows = [half]
        self.first = [0]
        for s, a in zip(self.sizes, self.digits):
            self.rows.append(self.rows[-1] // s)
            self.first.append(self.first[-1] + a * self.rows[-1])

def sum_kernel(chips, lags, live, left, right, high, low, *scratch):
    lefts, rights, turned, masked, part, arrived, acc, total = scratch[:8]
    p_in, q_in = scratch[8:11], scratch[11:14]
    fetched, d2d, fwd = scratch[14:17]
    rs, ag = scratch[17:20], scratch[20:23]
    qrs, qag = scratch[23:26], scratch[26:29]
    me = lax.axis_index("rows")
    core = lax.rem(me, 2)
    chip = me // 2
    partner = me + 1 - 2 * core
    chunks, size = part.shape[:2]
    half = size // 2
    tile_rows = left.shape[0] // SLOTS
    blocks = size // PANEL
    kx, ky, kz = grid_of(chips)
    flat = kx == ky
    def pick(c, a, b):
        return a + c * (b - a) if flat else a
    def axes(c, z_first):
        plane = [(kx, pick(c, 1, kx)), (ky, pick(c, kx, 1))]
        line = (kz, kx * ky)
        return [line] + plane if z_first else plane + [line]
    mine = {z: Route(chip, core, axes(core, z), half, 0) for z in (False, True)}
    theirs = {z: Route(chip, core, axes(1 - core, z), half, 0) for z in (False, True)}

    def lanes(c):
        return pl.ds(c * LANES if isinstance(c, int) else pl.multiple_of(c * LANES, LANES), LANES)
    def rows(start, count, base=0):
        return pl.ds(pl.multiple_of(base + start, GROUP), count)
    def copy(src, dst, send, recv, device):
        return pltpu.make_async_remote_copy(src_ref=src, dst_ref=dst, send_sem=send, recv_sem=recv, device_id=(device,), device_id_type=MESH)

    my_base, its_base = core * half, (1 - core) * half

    def to_partner(c):
        return copy(part.at[c, rows(0, half, its_base)], arrived.at[c], d2d.at[0, c], d2d.at[1, c], partner)

    def peer(r, p, step):
        digit = lax.rem(r.digits[p] + step + r.sizes[p], r.sizes[p])
        return digit, 2 * (chip + (digit - r.digits[p]) * r.strides[p]) + core

    def rs_copy(z, p, c, u):
        r = mine[z]
        digit, device = peer(r, p, u)
        n = r.rows[p + 1]
        sems = (qrs if z else rs)[p]
        box = (q_in if z else p_in)[p]
        slot = 0 if z else c - 1
        return copy(acc.at[c, rows(r.first[p] + digit * n, n)], box.at[slot, u - 1], sems.at[0, slot, u - 1], sems.at[1, slot, u - 1], device)

    def ag_copy(z, p, c, u, outgoing):
        r = mine[z]
        n = r.rows[p + 1]
        digit, device = peer(r, p, u if outgoing else -u)
        where = rows(r.first[p + 1] if outgoing else r.first[p] + digit * n, n, my_base)
        sems = (qag if z else ag)[p]
        slot = 0 if z else c - 1
        return copy(total.at[c, where], total.at[c, where], sems.at[0, slot, u - 1], sems.at[1, slot, u - 1], device)

    def pieces(r, base):
        out = [rows(r.first[2], r.rows[2], base)]
        for p in (1, 0):
            for u in range(1, r.sizes[p]):
                digit = lax.rem(r.digits[p] - u + r.sizes[p], r.sizes[p])
                out.append(rows(r.first[p] + digit * r.rows[p + 1], r.rows[p + 1], base))
        return out

    def pass_on(z, c, i, outgoing):
        where = pieces(mine[z] if outgoing else theirs[z], my_base if outgoing else its_base)[i]
        return copy(total.at[c, where], total.at[c, where], fwd.at[0, c, i], fwd.at[1, c, i], partner)

    def put(c, where):
        pair = split(total[c, where, :])
        high[where, lanes(c)] = pair[0]
        low[where, lanes(c)] = pair[1]

    def rs_start(z, p, c):
        for u in range(1, mine[z].sizes[p]):
            rs_copy(z, p, c, u).start()

    def rs_finish(z, p, c):
        r = mine[z]
        for u in range(1, r.sizes[p]):
            rs_copy(z, p, c, u).wait_recv()
        where = rows(r.first[p + 1], r.rows[p + 1])
        box = (q_in if z else p_in)[p]
        slot = 0 if z else c - 1
        value = acc[c, where, :]
        for u in range(1, r.sizes[p]):
            value += box[slot, u - 1]
        if p == 2:
            total[c, rows(r.first[3], r.rows[3], my_base), :] = value
        else:
            acc[c, where, :] = value

    def ag_start(z, p, c):
        for u in range(1, mine[z].sizes[p]):
            ag_copy(z, p, c, u, True).start()

    def ag_finish(z, p, c):
        for u in range(1, mine[z].sizes[p]):
            ag_copy(z, p, c, u, False).wait_recv()

    def event(kind, z, c):
        if kind == "D":
            to_partner(c).wait_recv()
            acc[c] = part[c, rows(0, half, my_base), :] + arrived[c]
            rs_start(z, 0, c)
        elif kind in ("F1", "F2"):
            p = int(kind[1]) - 1
            rs_finish(z, p, c)
            rs_start(z, p + 1, c)
        elif kind == "F3":
            rs_finish(z, 2, c)
            ag_start(z, 2, c)
        elif kind == "A3":
            ag_finish(z, 2, c)
            ag_start(z, 1, c)
            pass_on(z, c, 0, True).start()
            put(c, pieces(mine[z], my_base)[0])
        elif kind == "A2":
            ag_finish(z, 1, c)
            ag_start(z, 0, c)
            for u in range(1, mine[z].sizes[1]):
                pass_on(z, c, u, True).start()
                put(c, pieces(mine[z], my_base)[u])
        elif kind == "A1":
            ag_finish(z, 0, c)
            for u in range(1, mine[z].sizes[0]):
                i = u + mine[z].sizes[1] - 1
                pass_on(z, c, i, True).start()
                put(c, pieces(mine[z], my_base)[i])
        else:
            for i, where in enumerate(pieces(theirs[z], its_base)):
                pass_on(z, c, i, False).wait_recv()
                put(c, where)

    def each(first, end, body):
        def step(u, carry):
            body(u)
            return carry
        lax.fori_loop(first, end, step, 0)

    barrier = pltpu.get_barrier_semaphore()
    pl.semaphore_signal(barrier, inc=1, device_id=(partner,), device_id_type=MESH)
    count = 1
    for p in range(3):
        for u in range(1, mine[False].sizes[p]):
            pl.semaphore_signal(barrier, inc=1, device_id=(peer(mine[False], p, u)[1],), device_id_type=MESH)
            count += 1
    pl.semaphore_wait(barrier, count)

    def fetch(s):
        where = pl.ds(pl.multiple_of(s * tile_rows, GROUP), tile_rows)
        slot = s % 2
        return (
            pltpu.make_async_copy(left.at[where], lefts.at[slot], fetched.at[0, s]),
            pltpu.make_async_copy(right.at[where], rights.at[slot], fetched.at[1, s]),
        )

    def fetch_start(s):
        for side in fetch(s):
            side.start()

    def product(n, m):
        one = lambda a, b: lax.dot_general(a, b, NN, preferred_element_type=jnp.float32)
        both = one(turned[m], masked[0, n])
        value = both[:PANEL] + (both[PANEL:] + one(turned[m, :PANEL], masked[1, n]))
        block = pl.ds(pl.multiple_of(m * PANEL, PANEL), PANEL)
        for h in range(PANEL // LANES):
            part[n * (PANEL // LANES) + h, block, :] = value[:, h * LANES : (h + 1) * LANES]

    def exchange(n):
        for h in range(PANEL // LANES):
            to_partner(n * (PANEL // LANES) + h).start()

    fetch_start(0)
    fetch_start(1)
    for s in range(SLOTS):
        for side in fetch(s):
            side.wait()
        mask = (s < live[0]).astype(jnp.float32)
        where = pl.ds(s * tile_rows, tile_rows)
        for m in range(blocks):
            lane = slice(m * PANEL, (m + 1) * PANEL)
            pair = split(rights[s % 2, :, lane] * mask)
            masked[0, m, where, :] = pair[0]
            masked[1, m, where, :] = pair[1]
            turn = split(lefts[s % 2, :, lane].T)
            turned[m, :PANEL, where] = turn[0]
            turned[m, PANEL:, where] = turn[1]
            if m == 0:
                first = pair
            value = dot_pairs(turn, first, NN)
            block = pl.ds(m * PANEL, PANEL)
            for h in range(PANEL // LANES):
                piece = value[:, h * LANES : (h + 1) * LANES]
                part[h, block, :] = piece if s == 0 else part[h, block, :] + piece
        if s + 2 < SLOTS:
            fetch_start(s + 2)
    exchange(0)

    q_lags = lags["Q"]
    stride = lags["stride"]
    kinds = ("F1", "F2", "F3", "A3", "A2", "A1", "W")
    steps = (blocks - 1) * blocks
    end = 1 + max(steps + lags["D"], lags["W"] + stride * (chunks - 1), q_lags["W"])

    def step(t):
        @pl.when(t < steps)
        def _():
            product(1 + t // blocks, lax.rem(t, blocks))

        @pl.when((t < steps) & (lax.rem(t, blocks) == blocks - 1))
        def _():
            exchange(1 + t // blocks)

        n = (t - lags["D"]) // blocks
        ready = (t >= lags["D"]) & (t <= steps + lags["D"]) & (lax.rem(t - lags["D"] + blocks, blocks) == 0)

        @pl.when(ready & (n == 0))
        def _():
            event("D", True, 0)
            for h in range(1, PANEL // LANES):
                event("D", False, h)

        @pl.when(ready & (n > 0))
        def _():
            for h in range(PANEL // LANES):
                event("D", False, n * (PANEL // LANES) + h)

        for kind in kinds:
            ahead = t - lags[kind]
            c = ahead // stride
            pl.when((ahead >= stride) & (c < chunks) & (lax.rem(ahead + stride, stride) == 0))(functools.partial(event, kind, False, c))
            pl.when(t == q_lags[kind])(functools.partial(event, kind, True, 0))

    each(0, end, step)

    def drain(z, c):
        to_partner(c).wait_send()
        for p in range(3):
            for u in range(1, mine[z].sizes[p]):
                rs_copy(z, p, c, u).wait_send()
                ag_copy(z, p, c, u, True).wait_send()
        for i in range(len(pieces(mine[z], my_base))):
            pass_on(z, c, i, True).wait_send()

    drain(True, 0)
    each(1, chunks, lambda c: drain(False, c))


LAGS = dict(stride=2, D=2, F1=7, F2=11, F3=15, A3=19, A2=23, A1=27, W=29, Q=dict(F1=12, F2=16, F3=19, A3=22, A2=25, A1=33, W=35))


def sum_over_devices(live, left, right, devices, lags=LAGS):
    chips = devices // 2
    rows, size = left.shape
    half = size // 2
    chunks = size // LANES
    blocks = size // PANEL
    tile_rows = rows // SLOTS
    kx, ky, kz = grid_of(chips)
    vmem = pl.BlockSpec(memory_space=pltpu.VMEM)
    smem = pl.BlockSpec(memory_space=pltpu.SMEM)
    hbm = pl.BlockSpec(memory_space=pl.ANY)
    dma = pltpu.SemaphoreType.DMA

    def boxes(order, slots):
        rest, out = half, []
        for k in order:
            rest //= k
            out.append(pltpu.VMEM((slots, k - 1, rest, LANES), jnp.float32))
        return out

    def sems(order, slots):
        return [dma((2, slots, k - 1)) for k in order]

    p_order, q_order = (kx, ky, kz), (kz, kx, ky)
    scratch = [pltpu.VMEM((2, tile_rows, size), jnp.float32)] * 2
    scratch += [pltpu.VMEM((blocks, 2 * PANEL, rows), jnp.bfloat16), pltpu.VMEM((2, blocks, rows, PANEL), jnp.bfloat16)]
    scratch += [pltpu.VMEM((chunks, size, LANES), jnp.float32)] + [pltpu.VMEM((chunks, half, LANES), jnp.float32)] * 2
    scratch += [pltpu.VMEM((chunks, size, LANES), jnp.float32)]
    scratch += boxes(p_order, chunks - 1) + boxes(q_order, 1)
    scratch += [dma((2, SLOTS)), dma((2, chunks)), dma((2, chunks, max(kx + ky - 1, kz + kx - 1)))]
    scratch += sems(p_order, chunks - 1) * 2 + sems(q_order, 1) * 2
    return pl.pallas_call(
        functools.partial(sum_kernel, chips, lags),
        out_shape=[jax.ShapeDtypeStruct((size, size), jnp.bfloat16)] * 2,
        in_specs=[smem, hbm, hbm],
        out_specs=[vmem, vmem],
        scratch_shapes=scratch,
        compiler_params=pltpu.CompilerParams(collective_id=0, has_side_effects=True, vmem_limit_bytes=48 * 2**20),
        name="gram_over_devices",
    )(live, left, right)


def inverse_factor(matrix, spread, beside):
    size = matrix.shape[0]
    groups = size // GROUP
    shape = (GROUP, size)
    row_ids = lax.broadcasted_iota(jnp.int32, shape, 0)
    lane_ids = lax.broadcasted_iota(jnp.int32, shape, 1)
    wide = lambda v: jnp.broadcast_to(v, shape)
    tiles = [matrix[GROUP * g : GROUP * (g + 1), :] for g in range(groups)]
    done = []
    for g in range(groups):
        first = GROUP * g
        columns = {r: [wide(tiles[r][:, first + j : first + j + 1]) for j in range(GROUP)] for r in range(g, groups)}
        for j in range(GROUP):
            spread[g, j] = columns[g][j]
        entry = {(i, j): spread[g, j, pl.ds(i, GROUP, stride=0), :] for j in range(GROUP) for i in range(j, GROUP)}
        here = (lane_ids >= first) & (lane_ids < first + GROUP)
        panel = jnp.where(here, jnp.where(lane_ids == row_ids + first, 1.0, 0.0), tiles[g])
        rows = [wide(panel[j : j + 1, :]) for j in range(GROUP)]
        factor, scale = {}, []
        for j in range(GROUP):
            scale.append(lax.rsqrt(entry[j, j]))
            rows[j] = rows[j] * scale[j]
            for i in range(j + 1, GROUP):
                factor[i, j] = entry[i, j] * scale[j]
            for l in range(j + 1, GROUP):
                for i in range(l, GROUP):
                    entry[i, l] = entry[i, l] - factor[i, j] * factor[l, j]
            for i in range(j + 1, GROUP):
                rows[i] = rows[i] - factor[i, j] * rows[j]
        beside(g)
        out = rows[0]
        for j in range(1, GROUP):
            out = jnp.where(row_ids == j, rows[j], out)
        done.append(jnp.where(lane_ids <= row_ids + first, out, 0.0))
        if g + 1 == groups:
            break
        solved = [rows[j] * scale[j] for j in range(GROUP)]
        rest = {r: jnp.where(here, 0.0, tiles[r]) for r in range(g + 1, groups)}
        for j in reversed(range(GROUP)):
            for l in range(j):
                solved[l] = solved[l] - (factor[j, l] * scale[l]) * solved[j]
            for r in range(g + 1, groups):
                rest[r] = rest[r] - columns[r][j] * solved[j]
        for r in rest:
            tiles[r] = rest[r]
    return jnp.concatenate(done, axis=0)


def maps_kernel(live, start, high, low, left, right, left_out, right_out, sides, products, now, image, after, square, inverse, earlier, spread, sems):
    rank = start.shape[1]
    cut = rank // 2
    rows = left.shape[0]
    tile_rows = rows // SLOTS
    fetch = [pltpu.make_async_copy(src, sides.at[i], sems.at[0, i]) for i, src in enumerate((left, right))]
    fetch[1].start()
    fetch[0].start()
    image[...] = dot_pairs(split(start[...].T), (high[...], low[...]), NT)
    now[...] = dot_pairs(split(image[...]), (high[...], low[...]), NN)
    inverse[...] = jnp.zeros_like(inverse)
    fetch[1].wait()
    fetch[0].wait()

    def turn(iteration, carry):
        side = jnp.where(iteration == POWER, 0, 1)
        pair = split(now[...])
        square[...] = dot_pairs(pair, pair, NT)

        def apply_gram(n):
            block = pl.ds(n * PANEL, PANEL)
            after[:, block] = dot_pairs(pair, (high[block, :], low[block, :]), NT)

        def apply_side(m):
            block = pl.ds(m * PANEL, PANEL)
            products[side, block, :] = dot_pairs(split(sides[side, block, :]), pair, NT)

        work = [functools.partial(apply_gram, n) for n in range(high.shape[0] // PANEL)]
        work += [functools.partial(apply_side, m) for m in range(rows // PANEL)]
        groups = cut // GROUP

        def beside(half, g):
            step = half * groups + g
            for job in work[step * len(work) // (2 * groups) : (step + 1) * len(work) // (2 * groups)]:
                job()

        first = inverse_factor(square[:cut, :cut], spread.at[0], functools.partial(beside, 0))
        across = full_dot(first, square[:cut, cut:])
        across_t = across.T
        second = inverse_factor(square[cut:, cut:] - full_dot(across_t, across), spread.at[1], functools.partial(beside, 1))
        inverse[:cut, :cut] = first
        inverse[cut:, cut:] = second
        inverse[cut:, :cut] = -full_dot(second, full_dot(across_t, first))

        @pl.when(iteration < POWER)
        def _():
            image[...] = dot_pairs(split(inverse[...]), split(after[...]), NN)

        @pl.when(iteration < POWER - 1)
        def _():
            now[...] = dot_pairs(split(image[...]), (high[...], low[...]), NN)

        @pl.when(iteration == POWER - 1)
        def _():
            now[...] = image[...]
            earlier[...] = inverse[...]

        return carry

    lax.fori_loop(0, POWER + 1, turn, 0)
    shape = square.shape
    diagonal = lax.broadcasted_iota(jnp.int32, shape, 0) == lax.broadcasted_iota(jnp.int32, shape, 1)
    trace = jnp.sum(jnp.where(diagonal, square[...], 0.0), keepdims=True)
    both = full_dot(inverse[...], earlier[...]) * jnp.sqrt(trace / rank)
    stores = []
    for side, (small, out) in enumerate(((inverse[...], left_out), (both, right_out))):
        small = split(small)
        for slot in range(SLOTS):
            block = pl.ds(slot * tile_rows, tile_rows)
            mask = (slot < live[0]).astype(jnp.float32)
            products[side, block, :] = dot_pairs(split(products[side, block, :]), small, NT) * mask
            stores.append(pltpu.make_async_copy(products.at[side, block], out.at[block], sems.at[1 + side, slot]))
            stores[-1].start()
    for store in stores:
        store.wait()


def project(left, right, live, start, high, low):
    states, rank = start.shape
    rows = left.shape[0]
    cut = rank // 2
    vmem = pl.BlockSpec(memory_space=pltpu.VMEM)
    smem = pl.BlockSpec(memory_space=pltpu.SMEM)
    hbm = pl.BlockSpec(memory_space=pl.ANY)
    small = pltpu.VMEM((rank, rank), jnp.float32)
    wide = pltpu.VMEM((rank, states), jnp.float32)
    return pl.pallas_call(
        maps_kernel,
        out_shape=[jax.ShapeDtypeStruct((rows, rank), jnp.float32)] * 2,
        in_specs=[smem, vmem, vmem, vmem, hbm, hbm],
        out_specs=[hbm, hbm],
        scratch_shapes=[
            pltpu.VMEM((2, rows, states), jnp.float32),
            pltpu.VMEM((2, rows, rank), jnp.float32),
            wide, wide, wide, small, small, small,
            pltpu.VMEM((2, cut // GROUP, GROUP, GROUP, cut), jnp.float32),
            pltpu.SemaphoreType.DMA((3, SLOTS)),
        ],
        compiler_params=pltpu.CompilerParams(vmem_limit_bytes=48 * 2**20),
        name="project",
    )(live, start, high, low, left, right)


def local(devices, left_factor, right_factor, tile_counts, start_basis):
    high, low = sum_over_devices(tile_counts, left_factor, right_factor, devices)
    return project(left_factor, right_factor, tile_counts, start_basis, high, low)


def solution(mesh):
    return jax.shard_map(
        functools.partial(local, mesh.shape["rows"]),
        mesh=mesh,
        in_specs=(P("rows", None), P("rows", None), P("rows"), P()),
        out_specs=(P("rows", None), P("rows", None)),
        check_vma=False,
    )
```

time: 152 us -> 112 us (0.74)
  matrix products: 32.4 us -> 0 us
  local copies, waits for them, and re-layouts: 9.13 us -> 0.01 us
    dot_general x3 -> x0, matrix products: 32.4 us -> none  [the longest x1 20.2 us: local(): lax.dot_general(left_factor, right_factor * row_mask, (((0,), (0,)), ((),...]
    pallas_call x1, Pallas kernels: 56.1 us -> 70.4 us  [sum_over_devices(): pl.pallas_call(functools.partial(sum_kernel, chips, lags), out_shape=[jax...]
    pallas_call x1, Pallas kernels: 53.1 us -> 39.9 us  [project(): pl.pallas_call(maps_kernel, out_shape=[jax.ShapeDtypeStruct((rows, rank),...]
    unnamed x13 -> x2, local copies, waits for them, and re-layouts: 9.13 us -> 0.01 us
where the time goes in v2:
time: 112 us
  Pallas kernels  110 us (98%)
  between operations  1.46 us (1%)
    pallas_call x1, Pallas kernels, sum_over_devices(): pl.pallas_call(functools.partial(sum_kernel, chips, lags), out_shape=[jax...  70.4 us
    pallas_call x1, Pallas kernels, project(): pl.pallas_call(maps_kernel, out_shape=[jax.ShapeDtypeStruct((rows, rank),...  39.9 us

profile of v2, /device:TPU:1, one launch (start us, length us, event | category | flops | bytes accessed | tf_op | source)
XLA Modules:
  0.0 111.7 jit_solution(16108081655405826482)
XLA Ops:
  1.3 0.0 copy-start
  1.3 70.4 %gram_over_devices.1 = (bf16[1024,1024]{1,0:T(8,128)(2,1)S(1)}, bf16[1024,1024]{1,0:T(8,128)(2,1)S(1)}) custom-call(s32[1]{0:T(128)S(6)} %copy.6.live, f32[2048,1024]{1,0:T(8,128)} %left.3, f32[2048,1024]{1,0:T(8,128)} %right.3), custom_call_target="tpu_custom_call" | custom-call | tf_op jit(solution)/shard_map/gram_over_devices/pallas_call | solution.py:342
  71.7 0.0 copy-done
  71.7 39.9 %project.1 = (f32[2048,256]{1,0:T(8,128)}, f32[2048,256]{1,0:T(8,128)}) custom-call(s32[1]{0:T(128)S(6)} %copy.6.live, f32[1024,256]{1,0:T(8,128)S(1)} %copy-done, bf16[1024,1024]{1,0:T(8,128)(2,1)S(1)} %get-tuple-element.4.high, bf16[1024,1024]{1,0:T(8,128)(2,1)S(1)} %get-tuple-element.5.low, f32[2048,1024]{1,0:T(8,128)} %left.3, f32[2048,1024]{1,0:T(8,128)} %right.3), custom_call_target="tpu_custom_call" | custom-call | tf_op jit(solution)/shard_map/project/pallas_call | solution.py:487
Async XLA Ops:
  1.3 70.4 %copy-start = (f32[1024,256]{1,0:T(8,128)S(1)}, f32[1024,256]{1,0:T(8,128)}, u32[]{:S(2)}) copy-start(f32[1024,256]{1,0:T(8,128)} %start.1) | copy-start | bytes 3145732

commit v3 on v2

--- a/solution.py
+++ b/solution.py
@@ -410,10 +410,14 @@
     now[...] = dot_pairs(split(image[...]), (high[...], low[...]), NN)
     inverse[...] = jnp.zeros_like(inverse)
     fetch[1].wait()
-    fetch[0].wait()
 
     def turn(iteration, carry):
         side = jnp.where(iteration == POWER, 0, 1)
+
+        @pl.when(iteration == POWER)
+        def _():
+            fetch[0].wait()
+
         pair = split(now[...])
         square[...] = dot_pairs(pair, pair, NT)
 

time: 112 us -> 110 us (0.982)
  Pallas kernels: 110 us -> 108 us
    pallas_call x1, Pallas kernels: 39.9 us -> 37.7 us  [project(): pl.pallas_call(maps_kernel, out_shape=[jax.ShapeDtypeStruct((rows, rank),...]
where the time goes in v3:
time: 110 us
  Pallas kernels  108 us (98%)
  between operations  1.46 us (1%)
    pallas_call x1, Pallas kernels, sum_over_devices(): pl.pallas_call(functools.partial(sum_kernel, chips, lags), out_shape=[jax...  70.4 us
    pallas_call x1, Pallas kernels, project(): pl.pallas_call(maps_kernel, out_shape=[jax.ShapeDtypeStruct((rows, rank),...  37.7 us

profile of v3, /device:TPU:1, one launch (start us, length us, event | category | flops | bytes accessed | tf_op | source)
XLA Modules:
  0.0 109.6 jit_solution(9136409607019437515)
XLA Ops:
  1.3 0.0 copy-start
  1.3 70.4 %gram_over_devices.1 = (bf16[1024,1024]{1,0:T(8,128)(2,1)S(1)}, bf16[1024,1024]{1,0:T(8,128)(2,1)S(1)}) custom-call(s32[1]{0:T(128)S(6)} %copy.6.live, f32[2048,1024]{1,0:T(8,128)} %left.3, f32[2048,1024]{1,0:T(8,128)} %right.3), custom_call_target="tpu_custom_call" | custom-call | tf_op jit(solution)/shard_map/gram_over_devices/pallas_call | solution.py:342
  71.7 0.0 copy-done
  71.7 37.7 %project.1 = (f32[2048,256]{1,0:T(8,128)}, f32[2048,256]{1,0:T(8,128)}) custom-call(s32[1]{0:T(128)S(6)} %copy.6.live, f32[1024,256]{1,0:T(8,128)S(1)} %copy-done, bf16[1024,1024]{1,0:T(8,128)(2,1)S(1)} %get-tuple-element.4.high, bf16[1024,1024]{1,0:T(8,128)(2,1)S(1)} %get-tuple-element.5.low, f32[2048,1024]{1,0:T(8,128)} %left.3, f32[2048,1024]{1,0:T(8,128)} %right.3), custom_call_target="tpu_custom_call" | custom-call | tf_op jit(solution)/shard_map/project/pallas_call | solution.py:491
Async XLA Ops:
  1.3 70.4 %copy-start = (f32[1024,256]{1,0:T(8,128)S(1)}, f32[1024,256]{1,0:T(8,128)}, u32[]{:S(2)}) copy-start(f32[1024,256]{1,0:T(8,128)} %start.1) | copy-start | bytes 3145732
